TPU v7x, 32 devices: a whole 2x2x4 slice. The times are simulated.
32 devices in a mesh: section: 4 (over y, x), seq: 2 (over core), tensor: 4 (over z).
Axes of the slice: x: 2, y: 2, z: 4, core: 2. Of those that a mesh axis runs over, the one named last changes fastest.
Arguments:
- states_in: bfloat16 [1, 256, 4608], P(None, 'seq', 'tensor'), may hold values from -100 to 100
- span_order: int32 [4], replicated, may hold values from 0 to 3, each once
- pre_gain: bfloat16 [4, 4608], P('section'), may hold values from 0.25 to 1.75
- w_query: bfloat16 [4, 4608, 4096], P('section', None, 'tensor'), may hold values from -0.09375 to 0.09375
- w_key: bfloat16 [4, 4608, 2048], P('section', None, 'tensor'), may hold values from -0.09375 to 0.09375
- w_value: bfloat16 [4, 4608, 2048], P('section', None, 'tensor'), may hold values from -0.09375 to 0.09375
- w_out: bfloat16 [4, 4096, 4608], P('section', 'tensor'), may hold values from -0.125 to 0.125
- post_gain: bfloat16 [4, 4608], P('section'), may hold values from 0.25 to 1.75
Outputs:
- states: bfloat16 [4, 1, 256, 4608], P('section', None, 'seq', 'tensor')
Inputs may be any that keep to these rules, and one draw needn't show every extreme that they name: Each span number appears once; row block j of 64 rows holds the tokens from position span_order[j] * 64 on.
All inputs are finite; a program needn't handle non-finite values.
Results may differ from a plain program's by a relative error of at most 0.024.
Values may be sent and summed in bfloat16 or wider, within the bound.
A program may use at most 128 MiB of HBM per device.

v0:
```python
import jax
import jax.numpy as jnp
from jax import lax
from jax.sharding import PartitionSpec as P

HEAD_DIM = 128
softcap_limit = 50.0
query_scale = 144.0 ** (-0.5)
epsilon = 1e-06
rotary_base = 10000.0


def from_behind(value, axis, steps):
    count = lax.axis_size(axis)
    first, last = (max(0, -steps), min(count, count - steps))
    return lax.ppermute(value, axis, [(source, source + steps) for source in range(first, last)])


def rotate(vectors, places):
    half_dim = vectors.shape[-1] // 2
    inverse = rotary_base ** (-(jnp.arange(half_dim, dtype=jnp.float32) * 2.0 / vectors.shape[-1]))
    angles = places.astype(jnp.float32)[:, None] * inverse[None, :]
    cos_part = jnp.cos(angles)[:, None, :]
    sin_part = jnp.sin(angles)[:, None, :]
    lower_half = vectors[..., :half_dim]
    upper_half = vectors[..., half_dim:]
    return jnp.concatenate(
        [
            lower_half * cos_part - upper_half * sin_part,
            upper_half * cos_part + lower_half * sin_part,
        ],
        axis=-1,
    )


def span_positions(first_row, row_total, order_table, span_rows):
    row_ids = first_row + jnp.arange(row_total, dtype=jnp.int32)
    blocks = row_ids // span_rows
    matches = blocks[:, None] == jnp.arange(order_table.shape[0], dtype=jnp.int32)[None, :]
    starts = jnp.sum(jnp.where(matches, order_table[None, :], 0), axis=1)
    return starts * span_rows + row_ids % span_rows


def body(states_in, span_order, pre_gain, w_query, w_key, w_value, w_out, post_gain):
    micro_count, row_count, width_part = states_in.shape
    model_width = pre_gain.shape[1]
    head_size = HEAD_DIM
    kv_local = w_key.shape[2] // head_size
    q_local = w_query.shape[2] // head_size
    group_size = q_local // kv_local
    span_rows = row_count // 2
    section_count = lax.axis_size("section")
    section_rank = lax.axis_index("section")
    seq_rank = lax.axis_index("seq")
    tensor_rank = lax.axis_index("tensor")
    tick_total = section_count + micro_count - 1
    query_places = span_positions(seq_rank * row_count, row_count, span_order, span_rows)
    gain_in = pre_gain[0].astype(jnp.float32)
    gain_out = post_gain[0].astype(jnp.float32)

    def layer(full_rows):
        stream = full_rows.astype(jnp.float32)
        normed = (
            stream * lax.rsqrt(jnp.mean(stream * stream, axis=1, keepdims=True) + epsilon) * gain_in
        ).astype(jnp.bfloat16)
        queries = jnp.dot(normed, w_query[0], preferred_element_type=jnp.float32).reshape(
            row_count, q_local, head_size
        )
        queries = (
            (rotate(queries, query_places) * query_scale)
            .astype(jnp.bfloat16)
            .reshape(row_count, kv_local, group_size, head_size)
        )
        key_rows = jnp.dot(normed, w_key[0], preferred_element_type=jnp.float32).reshape(
            row_count, kv_local, head_size
        )
        key_rows = (
            rotate(key_rows, query_places)
            .astype(jnp.bfloat16)
            .reshape(row_count, kv_local * head_size)
        )
        values = jnp.dot(normed, w_value[0], preferred_element_type=jnp.float32).astype(
            jnp.bfloat16
        )
        key_piece = lax.all_gather(key_rows, "seq", axis=0, tiled=True)
        value_piece = lax.all_gather(values, "seq", axis=0, tiled=True)
        key_count = key_piece.shape[0]
        key_places = span_positions(jnp.int32(0), key_count, span_order, span_rows)
        scores = jnp.einsum(
            "tkgd,pkd->kgtp",
            queries,
            key_piece.reshape(key_count, kv_local, head_size),
            preferred_element_type=jnp.float32,
        )
        capped = softcap_limit * jnp.tanh(scores / softcap_limit)
        allowed = key_places[None, :] <= query_places[:, None]
        weight = jnp.where(allowed[None, None], jnp.exp(capped), jnp.float32(0.0))
        totals = jnp.sum(weight, axis=3)
        numerator = jnp.einsum(
            "kgtp,pkd->tkgd",
            weight.astype(jnp.bfloat16),
            value_piece.reshape(key_count, kv_local, head_size),
            preferred_element_type=jnp.float32,
        )
        numerator, totals = (numerator, totals)
        attended = (
            (numerator / jnp.transpose(totals, (2, 0, 1))[..., None])
            .astype(jnp.bfloat16)
            .reshape(row_count, q_local * head_size)
        )
        partial_value = jnp.dot(attended, w_out[0], preferred_element_type=jnp.float32)
        projected = lax.psum(partial_value.astype(jnp.bfloat16), "tensor").astype(jnp.float32)
        scaling = lax.rsqrt(jnp.mean(projected * projected, axis=1, keepdims=True) + epsilon)
        new_full = (stream + projected * scaling * gain_out).astype(jnp.bfloat16)
        new_part = lax.dynamic_slice_in_dim(new_full, tensor_rank * width_part, width_part, 1)
        return (new_part, new_full)

    def take_micro(tick_index):
        return lax.dynamic_index_in_dim(
            states_in, jnp.minimum(tick_index, micro_count - 1), 0, keepdims=False
        )

    def tick(carried, tick_index):
        outgoing, record = carried
        arrived = from_behind(outgoing, "section", 1)
        entering = lax.all_gather(take_micro(tick_index), "tensor", axis=1, tiled=True)
        full_rows = jnp.where(section_rank == 0, entering, arrived)
        new_part, new_full = layer(full_rows)
        slot_index = tick_index - section_rank
        is_valid = jnp.logical_and(slot_index >= 0, slot_index < micro_count)
        placed = lax.dynamic_update_index_in_dim(
            record, new_part, jnp.clip(slot_index, 0, micro_count - 1), 0
        )
        record = jnp.where(is_valid, placed, record)
        outgoing = new_full
        return ((outgoing, record), None)

    first_out = jnp.zeros((row_count, model_width), jnp.bfloat16)
    first_record = jnp.zeros((micro_count, row_count, width_part), jnp.bfloat16)
    (last_out, record), unused = lax.scan(
        tick, (first_out, first_record), jnp.arange(tick_total, dtype=jnp.int32)
    )
    return record[None]


def solution(mesh):
    in_specs = (
        P(None, "seq", "tensor"),
        P(),
        P("section", None),
        P("section", None, "tensor"),
        P("section", None, "tensor"),
        P("section", None, "tensor"),
        P("section", "tensor", None),
        P("section", None),
    )
    out_specs = P("section", None, "seq", "tensor")
    return jax.shard_map(body, mesh=mesh, in_specs=in_specs, out_specs=out_specs, check_vma=False)
```

profile of v0, /device:TPU:0, one launch (start us, length us, event | category | flops | bytes accessed | tf_op | source)
XLA Modules:
  0.0 498.4 jit_solution(17398841147142758691)
XLA Ops:
  8.8 12.7 %copy.28 = bf16[1,4608,1024]{1,2,0:T(8,128)(2,1)} copy(bf16[1,4608,1024]{2,1,0:T(8,128)(2,1)} %param.13) | data formatting | bytes 18874368
  21.5 6.8 %copy.27 = bf16[1,4608,512]{1,2,0:T(8,128)(2,1)} copy(bf16[1,4608,512]{2,1,0:T(8,128)(2,1)} %param.14) | data formatting | bytes 9437184
  28.3 462.6 %while.15 = (s32[]{:T(128)}, bf16[128,4608]{1,0:T(8,128)(2,1)S(1)}, bf16[1,128,1152]{2,1,0:T(8,128)(2,1)S(1)}, pred[]{:T(512)}, bf16[1,128,1152]{2,1,0:T(8,128)(...) while((s32[]{:T(128)}, bf16[128,4608]{1,0:T(8,128)(2,1)S(1)}, ...), condition=%wide.region_7.8_spmd.clone, body=%wide.region_1.7_spmd.clone.sunk | while | flops 3777902848 | bytes 106681320 | solution.py:140
  29.2 4.9 collective-permute-start
  34.5 24.7 %collective-permute-done = bf16[128,4608]{1,0:T(8,128)(2,1)S(1)} collective-permute-done((bf16[128,4608]{1,0:T(8,128)(2,1)S(1)}, bf16[128,4608]{1,0:T(8,128)(2,1)S(1)}, u32[]{:S(2)}, u32[]{:S(2)}) %collective-permute-start) | collective-permute-done | bytes 1179680 | tf_op jit(solution)/shard_map/while/body/eval_jaxpr/ppermute | solution.py:16
  59.2 4.3 all-gather.6.cloned.1.call-done
  63.6 1.9 fusion.82
  65.5 4.2 fusion.84
  69.8 2.0 all_gather.23
  71.8 2.7 fusion.85
  75.0 3.2 fusion.83
  78.2 2.0 all_gather.22
  81.2 6.2 %fusion.89 = bf16[128,4608]{1,0:T(8,128)(2,1)} fusion(bf16[128,1024]{0,1:T(8,128)(2,1)S(1)} %bitcast.117, bf16[1,1024,4608]{2,1,0:T(8,128)(2,1)} %get-tuple-element.538), kind=kOutput, calls=%fused_computation.2.clone.1 | convolution fusion | flops 1208549376 | bytes 10878976 | tf_op jit(solution)/shard_map/while/body/eval_jaxpr/dot_general | solution.py:111
  88.7 54.2 %all-reduce.2.cloned.1.call-done = bf16[128,4608]{1,0:T(8,128)(2,1)} async-done(((bf16[128,4608]{1,0:T(8,128)(2,1)}), bf16[128,4608]{1,0:T(8,128)(2,1)}) %all-reduce.2.cloned.1.call-update) | async-done | bytes 1179664 | tf_op jit(solution)/shard_map/while/body/eval_jaxpr/psum | solution.py:112
  147.3 3.4 collective-permute-start
  151.2 24.8 %collective-permute-done = bf16[128,4608]{1,0:T(8,128)(2,1)S(1)} collective-permute-done((bf16[128,4608]{1,0:T(8,128)(2,1)S(1)}, bf16[128,4608]{1,0:T(8,128)(2,1)S(1)}, u32[]{:S(2)}, u32[]{:S(2)}) %collective-permute-start) | collective-permute-done | bytes 1179680 | tf_op jit(solution)/shard_map/while/body/eval_jaxpr/ppermute | solution.py:16
  176.0 2.4 all-gather.6.cloned.1.call-done
  178.5 1.9 fusion.82
  180.4 4.2 fusion.84
  184.7 2.0 all_gather.23
  186.8 2.7 fusion.85
  189.9 3.2 fusion.83
  193.1 2.0 all_gather.22
  196.1 6.2 %fusion.89 = bf16[128,4608]{1,0:T(8,128)(2,1)} fusion(bf16[128,1024]{0,1:T(8,128)(2,1)S(1)} %bitcast.117, bf16[1,1024,4608]{2,1,0:T(8,128)(2,1)} %get-tuple-element.538), kind=kOutput, calls=%fused_computation.2.clone.1 | convolution fusion | flops 1208549376 | bytes 10878976 | tf_op jit(solution)/shard_map/while/body/eval_jaxpr/dot_general | solution.py:111
  203.6 54.2 %all-reduce.2.cloned.1.call-done = bf16[128,4608]{1,0:T(8,128)(2,1)} async-done(((bf16[128,4608]{1,0:T(8,128)(2,1)}), bf16[128,4608]{1,0:T(8,128)(2,1)}) %all-reduce.2.cloned.1.call-update) | async-done | bytes 1179664 | tf_op jit(solution)/shard_map/while/body/eval_jaxpr/psum | solution.py:112
  262.1 3.4 collective-permute-start
  266.0 24.8 %collective-permute-done = bf16[128,4608]{1,0:T(8,128)(2,1)S(1)} collective-permute-done((bf16[128,4608]{1,0:T(8,128)(2,1)S(1)}, bf16[128,4608]{1,0:T(8,128)(2,1)S(1)}, u32[]{:S(2)}, u32[]{:S(2)}) %collective-permute-start) | collective-permute-done | bytes 1179680 | tf_op jit(solution)/shard_map/while/body/eval_jaxpr/ppermute | solution.py:16
  290.8 2.3 all-gather.6.cloned.1.call-done
  293.1 1.9 fusion.82
  295.0 4.2 fusion.84
  299.3 2.0 all_gather.23
  301.3 2.7 fusion.85
  304.5 3.2 fusion.83
  307.7 2.0 all_gather.22
  310.7 6.2 %fusion.89 = bf16[128,4608]{1,0:T(8,128)(2,1)} fusion(bf16[128,1024]{0,1:T(8,128)(2,1)S(1)} %bitcast.117, bf16[1,1024,4608]{2,1,0:T(8,128)(2,1)} %get-tuple-element.538), kind=kOutput, calls=%fused_computation.2.clone.1 | convolution fusion | flops 1208549376 | bytes 10878976 | tf_op jit(solution)/shard_map/while/body/eval_jaxpr/dot_general | solution.py:111
  318.2 54.2 %all-reduce.2.cloned.1.call-done = bf16[128,4608]{1,0:T(8,128)(2,1)} async-done(((bf16[128,4608]{1,0:T(8,128)(2,1)}), bf16[128,4608]{1,0:T(8,128)(2,1)}) %all-reduce.2.cloned.1.call-update) | async-done | bytes 1179664 | tf_op jit(solution)/shard_map/while/body/eval_jaxpr/psum | solution.py:112
  374.0 1.8 fusion.91
  376.9 3.4 collective-permute-start
  380.7 24.8 %collective-permute-done = bf16[128,4608]{1,0:T(8,128)(2,1)S(1)} collective-permute-done((bf16[128,4608]{1,0:T(8,128)(2,1)S(1)}, bf16[128,4608]{1,0:T(8,128)(2,1)S(1)}, u32[]{:S(2)}, u32[]{:S(2)}) %collective-permute-start) | collective-permute-done | bytes 1179680 | tf_op jit(solution)/shard_map/while/body/eval_jaxpr/ppermute | solution.py:16
  405.6 2.4 all-gather.6.cloned.1.call-done
  408.0 1.9 fusion.82
  409.9 4.2 fusion.84
  414.2 2.0 all_gather.23
  416.3 2.7 fusion.85
  419.4 3.2 fusion.83
  422.6 2.0 all_gather.22
  425.6 6.2 %fusion.89 = bf16[128,4608]{1,0:T(8,128)(2,1)} fusion(bf16[128,1024]{0,1:T(8,128)(2,1)S(1)} %bitcast.117, bf16[1,1024,4608]{2,1,0:T(8,128)(2,1)} %get-tuple-element.538), kind=kOutput, calls=%fused_computation.2.clone.1 | convolution fusion | flops 1208549376 | bytes 10878976 | tf_op jit(solution)/shard_map/while/body/eval_jaxpr/dot_general | solution.py:111
  433.1 54.2 %all-reduce.2.cloned.1.call-done = bf16[128,4608]{1,0:T(8,128)(2,1)} async-done(((bf16[128,4608]{1,0:T(8,128)(2,1)}), bf16[128,4608]{1,0:T(8,128)(2,1)}) %all-reduce.2.cloned.1.call-update) | async-done | bytes 1179664 | tf_op jit(solution)/shard_map/while/body/eval_jaxpr/psum | solution.py:112
  (143 shorter events, 29.0 us)
Async XLA Ops:
  21.5 6.8 %copy-start.5 = (s32[4]{0:T(128)S(1)}, s32[4]{0:T(128)}, u32[]{:S(2)}) copy-start(s32[4]{0:T(128)} %param.11) | copy-start | bytes 52
  28.3 46.7 %copy-start.3 = (f32[4608]{0:T(1024)}, f32[4608]{0:T(1024)S(1)}, u32[]{:S(2)}) copy-start(f32[4608]{0:T(1024)S(1)} %get-tuple-element.531) | copy-start | bytes 55300 | tf_op jit(solution)/shard_map/while
  28.3 35.3 %all-gather.6.cloned.1.call-start = ((), (), s32[]{:S(2)}) async-start(), calls=%async_computation | async-start | bytes 1474560 | tf_op jit(solution)/shard_map/while/body/eval_jaxpr/all_gather | solution.py:126
  29.0 113.9 %all-reduce.2.cloned.1.call-start = ((), (), s32[]{:S(2)}) async-start(), calls=%async_computation.1 | async-start | bytes 2359296 | tf_op jit(solution)/shard_map/while/body/eval_jaxpr/psum | solution.py:112
  29.2 30.1 %collective-permute-start = (bf16[128,4608]{1,0:T(8,128)(2,1)S(1)}, bf16[128,4608]{1,0:T(8,128)(2,1)S(1)}, u32[]{:S(2)}, u32[]{:S(2)}) collective-permute-start(bf16[128,4608]{1,0:T(8,128)(2,1)S(1)} %broadcast_select_fusion.2), channel_id=1, source_target_pairs={{0,8},{8,16},{16,24},{1,9},{9,17},{17,25},{2,10},{10,18},{18,26},{... | collective-permute-start | bytes 3538952 | tf_op jit(solution)/shard_map/while/body/eval_jaxpr/ppermute | solution.py:16
  63.6 8.3 %copy-start = (bf16[1,4608,1024]{1,2,0:T(8,128)(2,1)S(1)}, bf16[1,4608,1024]{1,2,0:T(8,128)(2,1)}, u32[]{:S(2)}) copy-start(bf16[1,4608,1024]{1,2,0:T(8,128)(2,1)} %get-tuple-element.537) | copy-start | bytes 28311556 | tf_op jit(solution)/shard_map/while
  87.4 57.1 %copy-start.2 = (f32[4608]{0:T(1024)S(1)}, f32[4608]{0:T(1024)}, u32[]{:S(2)}) copy-start(f32[4608]{0:T(1024)} %get-tuple-element.539) | copy-start | bytes 55300 | tf_op jit(solution)/shard_map/while
  144.5 1.9 copy-start.4
  146.5 43.5 %copy-start.3 = (f32[4608]{0:T(1024)}, f32[4608]{0:T(1024)S(1)}, u32[]{:S(2)}) copy-start(f32[4608]{0:T(1024)S(1)} %get-tuple-element.531) | copy-start | bytes 55300 | tf_op jit(solution)/shard_map/while
  146.5 32.0 %all-gather.6.cloned.1.call-start = ((), (), s32[]{:S(2)}) async-start(), calls=%async_computation | async-start | bytes 1474560 | tf_op jit(solution)/shard_map/while/body/eval_jaxpr/all_gather | solution.py:126
  147.2 110.6 %all-reduce.2.cloned.1.call-start = ((), (), s32[]{:S(2)}) async-start(), calls=%async_computation.1 | async-start | bytes 2359296 | tf_op jit(solution)/shard_map/while/body/eval_jaxpr/psum | solution.py:112
  147.3 28.7 %collective-permute-start = (bf16[128,4608]{1,0:T(8,128)(2,1)S(1)}, bf16[128,4608]{1,0:T(8,128)(2,1)S(1)}, u32[]{:S(2)}, u32[]{:S(2)}) collective-permute-start(bf16[128,4608]{1,0:T(8,128)(2,1)S(1)} %broadcast_select_fusion.2), channel_id=1, source_target_pairs={{0,8},{8,16},{16,24},{1,9},{9,17},{17,25},{2,10},{10,18},{18,26},{... | collective-permute-start | bytes 3538952 | tf_op jit(solution)/shard_map/while/body/eval_jaxpr/ppermute | solution.py:16
  178.5 8.3 %copy-start = (bf16[1,4608,1024]{1,2,0:T(8,128)(2,1)S(1)}, bf16[1,4608,1024]{1,2,0:T(8,128)(2,1)}, u32[]{:S(2)}) copy-start(bf16[1,4608,1024]{1,2,0:T(8,128)(2,1)} %get-tuple-element.537) | copy-start | bytes 28311556 | tf_op jit(solution)/shard_map/while
  202.3 57.1 %copy-start.2 = (f32[4608]{0:T(1024)S(1)}, f32[4608]{0:T(1024)}, u32[]{:S(2)}) copy-start(f32[4608]{0:T(1024)} %get-tuple-element.539) | copy-start | bytes 55300 | tf_op jit(solution)/shard_map/while
  259.4 1.9 copy-start.4
  261.4 43.2 %copy-start.3 = (f32[4608]{0:T(1024)}, f32[4608]{0:T(1024)S(1)}, u32[]{:S(2)}) copy-start(f32[4608]{0:T(1024)S(1)} %get-tuple-element.531) | copy-start | bytes 55300 | tf_op jit(solution)/shard_map/while
  261.4 31.7 %all-gather.6.cloned.1.call-start = ((), (), s32[]{:S(2)}) async-start(), calls=%async_computation | async-start | bytes 1474560 | tf_op jit(solution)/shard_map/while/body/eval_jaxpr/all_gather | solution.py:126
  262.0 110.5 %all-reduce.2.cloned.1.call-start = ((), (), s32[]{:S(2)}) async-start(), calls=%async_computation.1 | async-start | bytes 2359296 | tf_op jit(solution)/shard_map/while/body/eval_jaxpr/psum | solution.py:112
  262.1 28.7 %collective-permute-start = (bf16[128,4608]{1,0:T(8,128)(2,1)S(1)}, bf16[128,4608]{1,0:T(8,128)(2,1)S(1)}, u32[]{:S(2)}, u32[]{:S(2)}) collective-permute-start(bf16[128,4608]{1,0:T(8,128)(2,1)S(1)} %broadcast_select_fusion.2), channel_id=1, source_target_pairs={{0,8},{8,16},{16,24},{1,9},{9,17},{17,25},{2,10},{10,18},{18,26},{... | collective-permute-start | bytes 3538952 | tf_op jit(solution)/shard_map/while/body/eval_jaxpr/ppermute | solution.py:16
  293.1 8.3 %copy-start = (bf16[1,4608,1024]{1,2,0:T(8,128)(2,1)S(1)}, bf16[1,4608,1024]{1,2,0:T(8,128)(2,1)}, u32[]{:S(2)}) copy-start(bf16[1,4608,1024]{1,2,0:T(8,128)(2,1)} %get-tuple-element.537) | copy-start | bytes 28311556 | tf_op jit(solution)/shard_map/while
  316.9 57.1 %copy-start.2 = (f32[4608]{0:T(1024)S(1)}, f32[4608]{0:T(1024)}, u32[]{:S(2)}) copy-start(f32[4608]{0:T(1024)} %get-tuple-element.539) | copy-start | bytes 55300 | tf_op jit(solution)/shard_map/while
  374.0 1.9 copy-start.4
  375.9 43.5 %copy-start.3 = (f32[4608]{0:T(1024)}, f32[4608]{0:T(1024)S(1)}, u32[]{:S(2)}) copy-start(f32[4608]{0:T(1024)S(1)} %get-tuple-element.531) | copy-start | bytes 55300 | tf_op jit(solution)/shard_map/while
  376.0 32.0 %all-gather.6.cloned.1.call-start = ((), (), s32[]{:S(2)}) async-start(), calls=%async_computation | async-start | bytes 1474560 | tf_op jit(solution)/shard_map/while/body/eval_jaxpr/all_gather | solution.py:126
  376.7 110.6 %all-reduce.2.cloned.1.call-start = ((), (), s32[]{:S(2)}) async-start(), calls=%async_computation.1 | async-start | bytes 2359296 | tf_op jit(solution)/shard_map/while/body/eval_jaxpr/psum | solution.py:112
  376.9 28.7 %collective-permute-start = (bf16[128,4608]{1,0:T(8,128)(2,1)S(1)}, bf16[128,4608]{1,0:T(8,128)(2,1)S(1)}, u32[]{:S(2)}, u32[]{:S(2)}) collective-permute-start(bf16[128,4608]{1,0:T(8,128)(2,1)S(1)} %broadcast_select_fusion.2), channel_id=1, source_target_pairs={{0,8},{8,16},{16,24},{1,9},{9,17},{17,25},{2,10},{10,18},{18,26},{... | collective-permute-start | bytes 3538952 | tf_op jit(solution)/shard_map/while/body/eval_jaxpr/ppermute | solution.py:16
  408.0 8.3 %copy-start = (bf16[1,4608,1024]{1,2,0:T(8,128)(2,1)S(1)}, bf16[1,4608,1024]{1,2,0:T(8,128)(2,1)}, u32[]{:S(2)}) copy-start(bf16[1,4608,1024]{1,2,0:T(8,128)(2,1)} %get-tuple-element.537) | copy-start | bytes 28311556 | tf_op jit(solution)/shard_map/while
  431.8 57.1 %copy-start.2 = (f32[4608]{0:T(1024)S(1)}, f32[4608]{0:T(1024)}, u32[]{:S(2)}) copy-start(f32[4608]{0:T(1024)} %get-tuple-element.539) | copy-start | bytes 55300 | tf_op jit(solution)/shard_map/while
  488.9 1.9 copy-start.4
  490.8 0.7 copy-start.1
Sparse Core Ops, SparseCore 0:
  30.7 32.8 all-gather.5
  87.6 55.3 all-reduce.1
  148.9 29.5 all-gather.5
  202.5 55.3 all-reduce.1
  263.5 29.5 all-gather.5
  317.1 55.3 all-reduce.1
  378.4 29.5 all-gather.5
  432.0 55.3 all-reduce.1
where the time goes:
time: 500 us; the launch traced here: 498 us
  waiting for transfers between devices  330 us (66%)
  matrix products  68.5 us (14%)
  other arithmetic  26.3 us (5%)
  local copies, waits for them, and re-layouts  25 us (5%)
  blocking collectives  16.1 us (3%)
  starting transfers between devices  15.6 us (3%)
  between operations  13.4 us (3%)
    psum x4, waiting for transfers between devices, layer(): lax.psum(partial_value.astype(jnp.bfloat16), 'tensor').astype(jnp.float32)  217 us
    ppermute x4, waiting for transfers between devices, from_behind(): lax.ppermute(value, axis, [(source, source + steps) for source in range(f...  99.1 us
    dot_general x4, matrix products, layer(): jnp.dot(attended, w_out[0], preferred_element_type=jnp.float32)  24.7 us
    unnamed x6, local copies, waits for them, and re-layouts  20.2 us
    dot_general x4, matrix products, layer(): jnp.dot(normed, w_key[0], preferred_element_type=jnp.float32)  16.9 us
    ppermute x4, starting transfers between devices, from_behind(): lax.ppermute(value, axis, [(source, source + steps) for source in range(f...  15.3 us
    dot_general x4, matrix products, layer(): jnp.dot(normed, w_value[0], preferred_element_type=jnp.float32)  12.6 us
    all_gather x4, waiting for transfers between devices, tick(): lax.all_gather(take_micro(tick_index), 'tensor', axis=1, tiled=True)  11.5 us
  transfers between devices with their start and end apart: 12, of which 12 were waited for; matrix products, arithmetic and copies ran while one was open for 1% of the time, Pallas kernels for 0%

commit v1 on v0

--- a/solution.py
+++ b/solution.py
@@ -109,7 +109,9 @@
             .reshape(row_count, q_local * head_size)
         )
         partial_value = jnp.dot(attended, w_out[0], preferred_element_type=jnp.float32)
-        projected = lax.psum(partial_value.astype(jnp.bfloat16), "tensor").astype(jnp.float32)
+        projected = jnp.sum(
+            lax.all_gather(partial_value.astype(jnp.bfloat16), "tensor"), axis=0
+        ).astype(jnp.float32)
         scaling = lax.rsqrt(jnp.mean(projected * projected, axis=1, keepdims=True) + epsilon)
         new_full = (stream + projected * scaling * gain_out).astype(jnp.bfloat16)
         new_part = lax.dynamic_slice_in_dim(new_full, tensor_rank * width_part, width_part, 1)

time: 500 us -> 641 us (1.28)
  waiting for transfers between devices: 330 us -> 460 us
    all_gather x0 -> x4, waiting for transfers between devices: none -> 350 us  [layer(): lax.all_gather(partial_value.astype(jnp.bfloat16), 'tensor')]
    psum x4 -> x0, waiting for transfers between devices: 217 us -> none  [layer(): lax.psum(partial_value.astype(jnp.bfloat16), 'tensor').astype(jnp.float32)]
    reduce_sum x0 -> x4, other arithmetic: none -> 12.6 us  [layer(): jnp.sum(lax.all_gather(partial_value.astype(jnp.bfloat16), 'tensor'), axi...]
    unnamed x6 -> x4, local copies, waits for them, and re-layouts: 20.2 us -> 19.5 us
where the time goes in v1:
time: 641 us; the launch traced here: 639 us
  waiting for transfers between devices  460 us (72%)
  matrix products  71.5 us (11%)
  other arithmetic  31.7 us (5%)
  local copies, waits for them, and re-layouts  27.1 us (4%)
  blocking collectives  16.1 us (3%)
  starting transfers between devices  15.5 us (2%)
  between operations  13.4 us (2%)
    all_gather x4, waiting for transfers between devices, layer(): lax.all_gather(partial_value.astype(jnp.bfloat16), 'tensor')  350 us
    ppermute x4, waiting for transfers between devices, from_behind(): lax.ppermute(value, axis, [(source, source + steps) for source in range(f...  98.6 us
    dot_general x4, matrix products, layer(): jnp.dot(attended, w_out[0], preferred_element_type=jnp.float32)  24.6 us
    unnamed x4, local copies, waits for them, and re-layouts  19.5 us
    dot_general x4, matrix products, layer(): jnp.dot(normed, w_key[0], preferred_element_type=jnp.float32)  17 us
    ppermute x4, starting transfers between devices, from_behind(): lax.ppermute(value, axis, [(source, source + steps) for source in range(f...  15.3 us
    dot_general x4, matrix products, layer(): jnp.dot(normed, w_query[0], preferred_element_type=jnp.float32)  13.5 us
  transfers between devices with their start and end apart: 12, of which 12 were waited for; matrix products, arithmetic and copies ran while one was open for 1% of the time, Pallas kernels for 0%

profile of v1, /device:TPU:0, one launch (start us, length us, event | category | flops | bytes accessed | tf_op | source)
XLA Modules:
  0.0 639.3 jit_solution(538585799848043186)
XLA Ops:
  8.8 12.7 %copy.28 = bf16[1,4608,1024]{1,2,0:T(8,128)(2,1)} copy(bf16[1,4608,1024]{2,1,0:T(8,128)(2,1)} %param.13) | data formatting | bytes 18874368
  21.5 6.8 %copy.27 = bf16[1,4608,512]{1,2,0:T(8,128)(2,1)} copy(bf16[1,4608,512]{2,1,0:T(8,128)(2,1)} %param.14) | data formatting | bytes 9437184
  28.3 604.2 %while.15 = (s32[]{:T(128)}, bf16[128,4608]{1,0:T(8,128)(2,1)S(1)}, bf16[1,128,1152]{2,1,0:T(8,128)(2,1)}, pred[]{:T(512)}, bf16[1,128,1152]{2,1,0:T(8,128)(2,1)...) while((s32[]{:T(128)}, bf16[128,4608]{1,0:T(8,128)(2,1)S(1)}, ...), condition=%wide.region_7.8_spmd.clone, body=%wide.region_1.7_spmd.clone.sunk | while | flops 3779082496 | bytes 125334480 | solution.py:142
  29.1 4.9 collective-permute-start
  34.5 24.7 %collective-permute-done = bf16[128,4608]{1,0:T(8,128)(2,1)S(1)} collective-permute-done((bf16[128,4608]{1,0:T(8,128)(2,1)S(1)}, bf16[128,4608]{1,0:T(8,128)(2,1)S(1)}, u32[]{:S(2)}, u32[]{:S(2)}) %collective-permute-start) | collective-permute-done | bytes 1179680 | tf_op jit(solution)/shard_map/while/body/eval_jaxpr/ppermute | solution.py:16
  59.2 4.3 all-gather.11.cloned.1.call-done
  63.6 1.9 fusion.82
  65.5 4.2 fusion.84
  69.8 2.0 all_gather.35
  71.9 3.4 fusion.85
  75.7 3.2 fusion.83
  78.9 2.0 all_gather.34
  82.0 6.2 fusion.89
  89.5 87.5 %all-gather.13.cloned.1.call-done = bf16[512,4608]{1,0:T(8,128)(2,1)} async-done(((bf16[128,4608]{1,0:T(8,128)(2,1)}), bf16[512,4608]{1,0:T(8,128)(2,1)}) %all-gather.13.cloned.1.call-update) | async-done | bytes 4718608 | tf_op jit(solution)/shard_map/while/body/eval_jaxpr/all_gather | solution.py:113
  177.1 3.1 reduce_sum.89
  183.5 3.4 collective-permute-start
  187.4 24.6 %collective-permute-done = bf16[128,4608]{1,0:T(8,128)(2,1)S(1)} collective-permute-done((bf16[128,4608]{1,0:T(8,128)(2,1)S(1)}, bf16[128,4608]{1,0:T(8,128)(2,1)S(1)}, u32[]{:S(2)}, u32[]{:S(2)}) %collective-permute-start) | collective-permute-done | bytes 1179680 | tf_op jit(solution)/shard_map/while/body/eval_jaxpr/ppermute | solution.py:16
  213.6 1.9 fusion.82
  215.6 4.2 fusion.84
  219.9 2.0 all_gather.35
  221.9 3.4 fusion.85
  225.8 3.2 fusion.83
  229.0 2.0 all_gather.34
  232.0 6.2 fusion.89
  239.6 87.5 %all-gather.13.cloned.1.call-done = bf16[512,4608]{1,0:T(8,128)(2,1)} async-done(((bf16[128,4608]{1,0:T(8,128)(2,1)}), bf16[512,4608]{1,0:T(8,128)(2,1)}) %all-gather.13.cloned.1.call-update) | async-done | bytes 4718608 | tf_op jit(solution)/shard_map/while/body/eval_jaxpr/all_gather | solution.py:113
  327.1 3.1 reduce_sum.89
  333.4 3.4 collective-permute-start
  337.3 24.6 %collective-permute-done = bf16[128,4608]{1,0:T(8,128)(2,1)S(1)} collective-permute-done((bf16[128,4608]{1,0:T(8,128)(2,1)S(1)}, bf16[128,4608]{1,0:T(8,128)(2,1)S(1)}, u32[]{:S(2)}, u32[]{:S(2)}) %collective-permute-start) | collective-permute-done | bytes 1179680 | tf_op jit(solution)/shard_map/while/body/eval_jaxpr/ppermute | solution.py:16
  363.4 1.9 fusion.82
  365.3 4.2 fusion.84
  369.6 2.0 all_gather.35
  371.6 3.4 fusion.85
  375.5 3.2 fusion.83
  378.7 2.0 all_gather.34
  381.8 6.2 fusion.89
  389.3 87.5 %all-gather.13.cloned.1.call-done = bf16[512,4608]{1,0:T(8,128)(2,1)} async-done(((bf16[128,4608]{1,0:T(8,128)(2,1)}), bf16[512,4608]{1,0:T(8,128)(2,1)}) %all-gather.13.cloned.1.call-update) | async-done | bytes 4718608 | tf_op jit(solution)/shard_map/while/body/eval_jaxpr/all_gather | solution.py:113
  476.8 3.1 reduce_sum.89
  483.3 3.4 collective-permute-start
  487.2 24.6 %collective-permute-done = bf16[128,4608]{1,0:T(8,128)(2,1)S(1)} collective-permute-done((bf16[128,4608]{1,0:T(8,128)(2,1)S(1)}, bf16[128,4608]{1,0:T(8,128)(2,1)S(1)}, u32[]{:S(2)}, u32[]{:S(2)}) %collective-permute-start) | collective-permute-done | bytes 1179680 | tf_op jit(solution)/shard_map/while/body/eval_jaxpr/ppermute | solution.py:16
  513.4 1.9 fusion.82
  515.3 4.2 fusion.84
  519.7 2.0 all_gather.35
  521.7 3.4 fusion.85
  525.6 3.2 fusion.83
  528.8 2.0 all_gather.34
  531.8 6.2 fusion.89
  539.4 87.5 %all-gather.13.cloned.1.call-done = bf16[512,4608]{1,0:T(8,128)(2,1)} async-done(((bf16[128,4608]{1,0:T(8,128)(2,1)}), bf16[512,4608]{1,0:T(8,128)(2,1)}) %all-gather.13.cloned.1.call-update) | async-done | bytes 4718608 | tf_op jit(solution)/shard_map/while/body/eval_jaxpr/all_gather | solution.py:113
  626.9 3.1 reduce_sum.89
  (137 shorter events, 30.3 us)
Async XLA Ops:
  21.5 6.8 %copy-start.3 = (s32[4]{0:T(128)S(1)}, s32[4]{0:T(128)}, u32[]{:S(2)}) copy-start(s32[4]{0:T(128)} %param.11) | copy-start | bytes 52
  28.3 35.3 %all-gather.11.cloned.1.call-start = ((), (), s32[]{:S(2)}) async-start(), calls=%async_computation | async-start | bytes 1474560 | tf_op jit(solution)/shard_map/while/body/eval_jaxpr/all_gather | solution.py:128
  29.0 148.1 %all-gather.13.cloned.1.call-start = ((), (), s32[]{:S(2)}) async-start(), calls=%async_computation.1 | async-start | bytes 5898240 | tf_op jit(solution)/shard_map/while/body/eval_jaxpr/all_gather | solution.py:113
  29.1 30.1 %collective-permute-start = (bf16[128,4608]{1,0:T(8,128)(2,1)S(1)}, bf16[128,4608]{1,0:T(8,128)(2,1)S(1)}, u32[]{:S(2)}, u32[]{:S(2)}) collective-permute-start(bf16[128,4608]{1,0:T(8,128)(2,1)S(1)} %broadcast_select_fusion.2), channel_id=1, source_target_pairs={{0,8},{8,16},{16,24},{1,9},{9,17},{17,25},{2,10},{10,18},{18,26},{... | collective-permute-start | bytes 3538952 | tf_op jit(solution)/shard_map/while/body/eval_jaxpr/ppermute | solution.py:16
  63.6 8.3 %copy-start = (bf16[1,4608,1024]{1,2,0:T(8,128)(2,1)S(1)}, bf16[1,4608,1024]{1,2,0:T(8,128)(2,1)}, u32[]{:S(2)}) copy-start(bf16[1,4608,1024]{1,2,0:T(8,128)(2,1)} %get-tuple-element.540) | copy-start | bytes 28311556 | tf_op jit(solution)/shard_map/while
  180.2 1.6 copy-start.1
  181.9 0.7 copy-start.2
  182.6 31.0 %all-gather.11.cloned.1.call-start = ((), (), s32[]{:S(2)}) async-start(), calls=%async_computation | async-start | bytes 1474560 | tf_op jit(solution)/shard_map/while/body/eval_jaxpr/all_gather | solution.py:128
  183.4 143.7 %all-gather.13.cloned.1.call-start = ((), (), s32[]{:S(2)}) async-start(), calls=%async_computation.1 | async-start | bytes 5898240 | tf_op jit(solution)/shard_map/while/body/eval_jaxpr/all_gather | solution.py:113
  183.5 28.5 %collective-permute-start = (bf16[128,4608]{1,0:T(8,128)(2,1)S(1)}, bf16[128,4608]{1,0:T(8,128)(2,1)S(1)}, u32[]{:S(2)}, u32[]{:S(2)}) collective-permute-start(bf16[128,4608]{1,0:T(8,128)(2,1)S(1)} %broadcast_select_fusion.2), channel_id=1, source_target_pairs={{0,8},{8,16},{16,24},{1,9},{9,17},{17,25},{2,10},{10,18},{18,26},{... | collective-permute-start | bytes 3538952 | tf_op jit(solution)/shard_map/while/body/eval_jaxpr/ppermute | solution.py:16
  213.6 8.3 %copy-start = (bf16[1,4608,1024]{1,2,0:T(8,128)(2,1)S(1)}, bf16[1,4608,1024]{1,2,0:T(8,128)(2,1)}, u32[]{:S(2)}) copy-start(bf16[1,4608,1024]{1,2,0:T(8,128)(2,1)} %get-tuple-element.540) | copy-start | bytes 28311556 | tf_op jit(solution)/shard_map/while
  330.3 1.6 copy-start.1
  332.0 0.7 copy-start.2
  332.7 30.7 %all-gather.11.cloned.1.call-start = ((), (), s32[]{:S(2)}) async-start(), calls=%async_computation | async-start | bytes 1474560 | tf_op jit(solution)/shard_map/while/body/eval_jaxpr/all_gather | solution.py:128
  333.3 143.6 %all-gather.13.cloned.1.call-start = ((), (), s32[]{:S(2)}) async-start(), calls=%async_computation.1 | async-start | bytes 5898240 | tf_op jit(solution)/shard_map/while/body/eval_jaxpr/all_gather | solution.py:113
  333.4 28.5 %collective-permute-start = (bf16[128,4608]{1,0:T(8,128)(2,1)S(1)}, bf16[128,4608]{1,0:T(8,128)(2,1)S(1)}, u32[]{:S(2)}, u32[]{:S(2)}) collective-permute-start(bf16[128,4608]{1,0:T(8,128)(2,1)S(1)} %broadcast_select_fusion.2), channel_id=1, source_target_pairs={{0,8},{8,16},{16,24},{1,9},{9,17},{17,25},{2,10},{10,18},{18,26},{... | collective-permute-start | bytes 3538952 | tf_op jit(solution)/shard_map/while/body/eval_jaxpr/ppermute | solution.py:16
  363.4 8.3 %copy-start = (bf16[1,4608,1024]{1,2,0:T(8,128)(2,1)S(1)}, bf16[1,4608,1024]{1,2,0:T(8,128)(2,1)}, u32[]{:S(2)}) copy-start(bf16[1,4608,1024]{1,2,0:T(8,128)(2,1)} %get-tuple-element.540) | copy-start | bytes 28311556 | tf_op jit(solution)/shard_map/while
  480.0 1.6 copy-start.1
  481.7 0.7 copy-start.2
  482.4 31.0 %all-gather.11.cloned.1.call-start = ((), (), s32[]{:S(2)}) async-start(), calls=%async_computation | async-start | bytes 1474560 | tf_op jit(solution)/shard_map/while/body/eval_jaxpr/all_gather | solution.py:128
  483.1 143.7 %all-gather.13.cloned.1.call-start = ((), (), s32[]{:S(2)}) async-start(), calls=%async_computation.1 | async-start | bytes 5898240 | tf_op jit(solution)/shard_map/while/body/eval_jaxpr/all_gather | solution.py:113
  483.3 28.5 %collective-permute-start = (bf16[128,4608]{1,0:T(8,128)(2,1)S(1)}, bf16[128,4608]{1,0:T(8,128)(2,1)S(1)}, u32[]{:S(2)}, u32[]{:S(2)}) collective-permute-start(bf16[128,4608]{1,0:T(8,128)(2,1)S(1)} %broadcast_select_fusion.2), channel_id=1, source_target_pairs={{0,8},{8,16},{16,24},{1,9},{9,17},{17,25},{2,10},{10,18},{18,26},{... | collective-permute-start | bytes 3538952 | tf_op jit(solution)/shard_map/while/body/eval_jaxpr/ppermute | solution.py:16
  513.4 8.3 %copy-start = (bf16[1,4608,1024]{1,2,0:T(8,128)(2,1)S(1)}, bf16[1,4608,1024]{1,2,0:T(8,128)(2,1)}, u32[]{:S(2)}) copy-start(bf16[1,4608,1024]{1,2,0:T(8,128)(2,1)} %get-tuple-element.540) | copy-start | bytes 28311556 | tf_op jit(solution)/shard_map/while
  630.0 1.6 copy-start.1
  631.7 0.7 copy-start.2
Sparse Core Ops, SparseCore 0:
  30.7 32.8 all-gather.10
  88.3 88.7 all-gather.12
  185.0 28.5 all-gather.10
  238.3 88.7 all-gather.12
  334.8 28.5 all-gather.10
  388.1 88.7 all-gather.12
  484.8 28.5 all-gather.10
  538.1 88.7 all-gather.12
